TPU v7x, 32 devices: a whole 2x2x4 slice. The times are simulated.
32 devices in a mesh: req: 8 (over z, core), blk: 4 (over y, x).
Axes of the slice: x: 2, y: 2, z: 4, core: 2. Of those that a mesh axis runs over, the one named last changes fastest.
Arguments:
- draft_node_queries: bfloat16 [256, 4096], P(('req', 'blk')), parts along dimension 0, may hold values from -6 to 6, as said below
- draft_node_keys: bfloat16 [256, 512], P(('req', 'blk')), parts along dimension 0, may hold values from -6 to 6
- draft_node_values: bfloat16 [256, 512], P(('req', 'blk')), parts along dimension 0, may hold values from -6 to 6
- paged_key_cache: bfloat16 [16384, 512], P(('req', 'blk')), parts along dimension 0, may hold values from -6 to 6
- paged_value_cache: bfloat16 [16384, 512], P(('req', 'blk')), parts along dimension 0, may hold values from -6 to 6
- context_length: int32 [8], P('req'), parts along dimension 0, may hold values from 1024 to 2048
- parents: int32 [256], P('req'), parts along dimension 0, may hold values from 0 to 31, as said below
- accepted_path: int32 [64], P('req'), parts along dimension 0, may hold values from 0 to 31, as said below
- out_weight: bfloat16 [2880, 4096], P('blk'), may hold values from -0.09375 to 0.09375
Outputs:
- tree_attention: bfloat16 [256, 4096], P(('req', 'blk')), parts along dimension 0
- path_output: bfloat16 [64, 2880], P('req', 'blk'), parts along dimension 0
There are 8 independent parts, one for each index of `req`. A program takes and returns all parts, laid end to end along the dimension named above; an argument that names none is the same for every part. Nothing has to cross between parts.
Inputs may be any that keep to these rules, and one draw needn't show every extreme that they name: `draft_node_queries`: query entries lie within the range. parents[0] = 0 marks the root; for i >= 1, parents[i] is one of the nodes i - 4 to i - 1 (and at least 0). `accepted_path`: distinct nodes; each entry after the first is a child of the one before it.
All inputs are finite; a program needn't handle non-finite values.
Results may differ from a plain program's by a relative error of at most 0.0095.
Values may be sent and summed in bfloat16 or wider, within the bound.
A program may use at most 64 MiB of HBM per device.

v0:
```python
import jax
import jax.numpy as jnp
from jax import lax
from jax.sharding import PartitionSpec as P

QUERY_HEADS = 64
KEY_VALUE_HEADS = 8
HEAD_WIDTH = 64
score_after_mask = -1e30


def ancestors(parents):
    draft_node_count = parents.shape[0]
    indices = jnp.arange(draft_node_count, dtype=jnp.int32)
    linked = (parents[:, None] == indices[None, :]) & (indices[:, None] > 0)
    ancestry = jnp.minimum(
        jnp.eye(draft_node_count, dtype=jnp.float32) + linked.astype(jnp.float32), 1.0
    )
    for squaring in range(7):
        ancestry = jnp.minimum(jnp.dot(ancestry, ancestry, precision=lax.Precision.HIGHEST), 1.0)
    return ancestry > 0.5


def fresh_state(cache_row_count):
    query_group_width = QUERY_HEADS // KEY_VALUE_HEADS
    return (
        jnp.full(
            (cache_row_count, KEY_VALUE_HEADS, query_group_width), score_after_mask, jnp.float32
        ),
        jnp.zeros((cache_row_count, KEY_VALUE_HEADS, query_group_width), jnp.float32),
        jnp.zeros((cache_row_count, KEY_VALUE_HEADS, query_group_width, HEAD_WIDTH), jnp.float32),
    )


def combine(first_part, second_part):
    maxima = jnp.maximum(first_part[0], second_part[0])
    first_scale = jnp.exp(first_part[0] - maxima)
    second_scale = jnp.exp(second_part[0] - maxima)
    totals = first_part[1] * first_scale + second_part[1] * second_scale
    weighted = first_part[2] * first_scale[..., None] + second_part[2] * second_scale[..., None]
    return (maxima, totals, weighted)


def fold_block(state, grouped_queries, flat_key_rows, flat_value_rows, usable):
    maxima, totals, weighted = state
    cache_row_count = flat_key_rows.shape[0]
    gathered_key_block = flat_key_rows.reshape(cache_row_count, KEY_VALUE_HEADS, HEAD_WIDTH)
    gathered_value_block = flat_value_rows.reshape(cache_row_count, KEY_VALUE_HEADS, HEAD_WIDTH)
    scores = jnp.einsum(
        "mrjz,xrz->mrjx", grouped_queries, gathered_key_block, preferred_element_type=jnp.float32
    ) * HEAD_WIDTH ** (-0.5)
    scores = jnp.where(usable, scores, score_after_mask)
    new_maxima = jnp.maximum(maxima, jnp.max(scores, axis=-1))
    weights = jnp.where(usable, jnp.exp(scores - new_maxima[..., None]), 0.0)
    rescale = jnp.exp(maxima - new_maxima)
    totals = totals * rescale + jnp.sum(weights, axis=-1)
    weighted = weighted * rescale[..., None] + jnp.einsum(
        "zvle,evt->zvlt",
        weights.astype(jnp.bfloat16),
        gathered_value_block,
        preferred_element_type=jnp.float32,
    )
    return (new_maxima, totals, weighted)


def cache_partial(grouped_queries, paged_key_cache, paged_value_cache, offset, length, state):
    rows_per_block = min(512, paged_key_cache.shape[0])
    block_table = paged_key_cache.shape[0] // rows_per_block
    gathered_key_blocks = paged_key_cache.reshape(
        block_table, rows_per_block, paged_key_cache.shape[1]
    )
    gathered_value_blocks = paged_value_cache.reshape(
        block_table, rows_per_block, paged_value_cache.shape[1]
    )
    starts = offset + rows_per_block * jnp.arange(block_table, dtype=jnp.int32)

    def step_fn(carried, pieces):
        usable = pieces[2] + jnp.arange(rows_per_block, dtype=jnp.int32) < length
        return (fold_block(carried, grouped_queries, pieces[0], pieces[1], usable), None)

    result, unused = lax.scan(step_fn, state, (gathered_key_blocks, gathered_value_blocks, starts))
    return result


def tree_partial(grouped_queries, keys_all, values_all, ancestry_rows):
    return fold_block(
        fresh_state(grouped_queries.shape[0]),
        grouped_queries,
        keys_all,
        values_all,
        ancestry_rows[:, None, None, :],
    )


def normalize(partial_value):
    cache_row_count = partial_value[2].shape[0]
    return (
        (partial_value[2] / partial_value[1][..., None])
        .astype(jnp.bfloat16)
        .reshape(cache_row_count, QUERY_HEADS * HEAD_WIDTH)
    )


def local(
    draft_node_queries,
    draft_node_keys,
    draft_node_values,
    paged_key_cache,
    paged_value_cache,
    context_length,
    parents,
    accepted_path,
    out_weight,
):
    own_rows = draft_node_queries.shape[0]
    draft_node_count = parents.shape[0]
    query_group_width = QUERY_HEADS // KEY_VALUE_HEADS
    position = lax.axis_index("blk")
    offset = position * paged_key_cache.shape[0]
    length = context_length[0]
    ancestry = ancestors(parents)
    own_ancestry = lax.dynamic_slice_in_dim(ancestry, position * own_rows, own_rows, 0)
    own_queries = draft_node_queries.reshape(
        own_rows, KEY_VALUE_HEADS, query_group_width, HEAD_WIDTH
    )
    every_query_row, keys_all, values_all = (
        lax.all_gather(draft_node_queries, "blk", axis=0, tiled=True),
        lax.all_gather(draft_node_keys, "blk", axis=0, tiled=True),
        lax.all_gather(draft_node_values, "blk", axis=0, tiled=True),
    )
    grouped_queries = every_query_row.reshape(
        draft_node_count, KEY_VALUE_HEADS, query_group_width, HEAD_WIDTH
    )
    partial_value = cache_partial(
        grouped_queries,
        paged_key_cache,
        paged_value_cache,
        offset,
        length,
        fresh_state(draft_node_count),
    )
    arrived = (
        lax.all_to_all(partial_value[0][None], "blk", split_axis=1, concat_axis=0, tiled=True),
        lax.all_to_all(partial_value[1][None], "blk", split_axis=1, concat_axis=0, tiled=True),
        lax.all_to_all(partial_value[2][None], "blk", split_axis=1, concat_axis=0, tiled=True),
    )
    maxima = jnp.max(arrived[0], axis=0)
    scales = jnp.exp(arrived[0] - maxima[None])
    totals = jnp.sum(arrived[1] * scales, axis=0)
    weighted = jnp.sum(arrived[2] * scales[..., None], axis=0)
    partial_value = combine(
        (maxima, totals, weighted), tree_partial(own_queries, keys_all, values_all, own_ancestry)
    )
    attention_own = normalize(partial_value)
    attention_all = lax.all_gather(attention_own, "blk", axis=0, tiled=True)
    picker = (
        accepted_path[:, None] == jnp.arange(draft_node_count, dtype=jnp.int32)[None, :]
    ).astype(jnp.bfloat16)
    path_rows = jnp.dot(picker, attention_all, preferred_element_type=jnp.float32).astype(
        jnp.bfloat16
    )
    path_output = lax.dot_general(
        path_rows, out_weight, (((1,), (1,)), ((), ())), preferred_element_type=jnp.float32
    ).astype(jnp.bfloat16)
    return (attention_own, path_output)


def solution(mesh):
    in_specs = (
        P(("req", "blk"), None),
        P(("req", "blk"), None),
        P(("req", "blk"), None),
        P(("req", "blk"), None),
        P(("req", "blk"), None),
        P("req"),
        P("req"),
        P("req"),
        P("blk", None),
    )
    out_specs = (P(("req", "blk"), None), P("req", "blk"))
    return jax.shard_map(local, mesh=mesh, in_specs=in_specs, out_specs=out_specs, check_vma=False)
```

profile of v0, /device:TPU:0, one launch (start us, length us, event | category | flops | bytes accessed | tf_op | source)
XLA Modules:
  0.0 78.9 jit_solution(13678298688536361862)
XLA Ops:
  1.3 10.8 %all_gather.12 = bf16[32,4096]{1,0:T(8,128)(2,1)S(1)} all-gather(bf16[8,4096]{1,0:T(8,128)(2,1)} %param.9), channel_id=1, replica_groups=mesh['req'=8,'blk'=4] {'blk'}, dimensions={0}, use_global_device_ids=true | all-gather | bytes 327680 | tf_op jit(solution)/shard_map/all_gather | solution.py:127
  12.0 0.5 reshape.137
  12.6 1.3 %copy.73 = bf16[512,512]{0,1:T(8,128)(2,1)S(1)} copy(bf16[512,512]{1,0:T(8,128)(2,1)} %param.12) | data formatting | bytes 1048576 | tf_op args[3]
  13.9 0.9 %bitcast_reduce_fusion = (f32[32,8,8]{0,2,1:T(8,128)S(1)}, f32[8,512,32,8]{1,2,3,0:T(8,128)S(1)}) fusion(pred[512]{0:T(512)(128)(4,1)S(1)} %add_compare_fusion, bf16[512,8,64,1]{0,2,3,1:T(8,128)(2,1)S(1)} %bitcast.85, bf16[32,8,8,64]{3,2,1,0:T(8,128)(2,1)S(1)} %reshape.137), kind=kOutput, calls=%fused_computation.2 | convolution fusion | flops 137361408 | bytes 4989440 | tf_op jit(solution)/shard_map/while/body/eval_jaxpr/mrjz,xrz->mrjx/dot_general | solution.py:49
  14.8 1.4 %fusion.2 = (f32[32,8,8]{0,2,1:T(8,128)S(1)}, bf16[32,8,8,512]{3,0,2,1:T(8,128)(2,1)S(1)}) fusion(f32[8,512,32,8]{1,2,3,0:T(8,128)S(1)} %get-tuple-element.41, f32[32,8,8]{0,2,1:T(8,128)S(1)} %get-tuple-element.39, pred[512]{0:T(512)(128)(4,1)S(1)} %add_compare_fusion), kind=kLoop, calls=%fused_computation.6 | loop fusion | flops 6289408 | bytes 6308352 | tf_op jit(solution)/shard_map/while/body/eval_jaxpr/reduce_sum | solution.py:56
  16.4 0.7 reshape.151
  17.1 3.2 %all-to-all-start.2 = ((f32[4,1,512]{2,1,0:T(1,128)}), f32[4,1,512]{2,1,0:T(1,128)S(1)}, u32[]{:S(2)}, u32[]{:S(2)}) async-start(f32[4,1,512]{2,1,0:T(1,128)} %reshape.151), calls=%async_computation.2 | async-start | bytes 16384 | tf_op jit(solution)/shard_map/all_to_all | solution.py:144
  20.4 0.2 reshape.140
  20.5 0.2 convolution_minimum_fusion.5
  20.9 0.1 convolution_minimum_fusion.3
  21.7 8.7 %all_gather.13 = bf16[32,512]{1,0:T(8,128)(2,1)S(1)} all-gather(bf16[8,512]{1,0:T(8,128)(2,1)S(1)} %copy-done.3), channel_id=1, replica_groups=mesh['req'=8,'blk'=4] {'blk'}, dimensions={0}, use_global_device_ids=true | all-gather | bytes 40960 | tf_op jit(solution)/shard_map/all_gather | solution.py:128
  30.5 0.3 fusion.54
  30.9 0.8 copy.75
  31.7 1.0 %copy.76 = bf16[512,512]{0,1:T(8,128)(2,1)} copy(bf16[512,512]{1,0:T(8,128)(2,1)S(1)} %copy-done) | data formatting | bytes 1048576 | tf_op args[4]
  32.7 2.4 %fusion.12 = f32[1,32,8,8,64]{4,3,1,2,0:T(8,128)S(1)} fusion(bf16[512,8,64,1]{0,2,3,1:T(8,128)(2,1)} %bitcast.91, bf16[32,8,8,512]{3,0,2,1:T(8,128)(2,1)S(1)} %get-tuple-element.26, f32[32,8,8]{2,0,1:T(8,128)} %copy.75), kind=kOutput, calls=%fused_computation.12 | convolution fusion | flops 134348800 | bytes 3153920 | tf_op jit(solution)/shard_map/while/body/eval_jaxpr/zvle,evt->zvlt/dot_general | solution.py:57
  35.1 0.3 fusion.26
  35.5 0.7 reshape.149
  36.4 1.4 %reshape.147 = f32[4,1,32768]{2,1,0:T(1,128)} reshape(f32[32,1,8,8,64]{4,3,2,1,0:T(8,128)S(1)} %bitcast.84) | data formatting | bytes 1048576
  37.9 3.2 %all-to-all-start.1 = ((f32[4,1,512]{2,1,0:T(1,128)}), f32[4,1,512]{2,1,0:T(1,128)S(1)}, u32[]{:S(2)}, u32[]{:S(2)}) async-start(f32[4,1,512]{2,1,0:T(1,128)} %reshape.149), calls=%async_computation.1 | async-start | bytes 16384 | tf_op jit(solution)/shard_map/all_to_all | solution.py:143
  41.1 8.6 %all_gather.14 = bf16[32,512]{1,0:T(8,128)(2,1)S(1)} all-gather(bf16[8,512]{1,0:T(8,128)(2,1)S(1)} %copy-done.4), channel_id=1, replica_groups=mesh['req'=8,'blk'=4] {'blk'}, dimensions={0}, use_global_device_ids=true | all-gather | bytes 40960 | tf_op jit(solution)/shard_map/all_gather | solution.py:129
  49.9 0.5 broadcast.122
  50.4 0.7 reduce.1
  51.2 3.5 %all-to-all-start = ((f32[4,1,32768]{2,1,0:T(1,128)}), f32[4,1,32768]{2,1,0:T(1,128)S(1)}, u32[]{:S(2)}, u32[]{:S(2)}) async-start(f32[4,1,32768]{2,1,0:T(1,128)} %reshape.147), calls=%async_computation | async-start | bytes 1048576 | tf_op jit(solution)/shard_map/all_to_all | solution.py:145
  54.7 0.7 reduce.2
  56.0 5.2 %all-to-all-done = f32[4,1,32768]{2,1,0:T(1,128)S(1)} async-done(((f32[4,1,32768]{2,1,0:T(1,128)}), f32[4,1,32768]{2,1,0:T(1,128)S(1)}, u32[]{:S(2)}, u32[]{:S(2)}) %all-to-all-start) | async-done | bytes 524320 | tf_op jit(solution)/shard_map/all_to_all | solution.py:145
  61.2 2.1 %reduce = f32[4,32768]{1,0:T(4,128)S(1)} reduce(f32[4,1,32768]{2,1,0:T(1,128)S(1)} %all-to-all-done, f32[]{:T(128)} %broadcast.122), dimensions={1}, to_apply=%all_to_all.12.reduce_sub_computation | reduce | bytes 1048580 | tf_op jit(solution)/shard_map/all_to_all | solution.py:145
  63.4 0.5 reshape.148
  63.9 0.3 multiply_reduce_fusion
  64.3 0.4 fusion.21
  64.7 0.2 reshape.142
  64.9 9.0 %all_gather.15 = bf16[32,4096]{1,0:T(8,128)(2,1)S(1)} all-gather(bf16[8,4096]{1,0:T(8,128)(2,1)S(1)} %reshape.142), channel_id=1, replica_groups=mesh['req'=8,'blk'=4] {'blk'}, dimensions={0}, use_global_device_ids=true | all-gather | bytes 327680 | tf_op jit(solution)/shard_map/all_gather | solution.py:155
  73.9 5.0 %fusion.23 = bf16[8,720]{1,0:T(8,128)(2,1)} fusion(bf16[720,4096]{1,0:T(8,128)(2,1)} %param.17, bf16[32,4096]{1,0:T(8,128)(2,1)S(1)} %all_gather.15, s32[8]{0:T(128)S(1)} %copy-done.5), kind=kOutput, calls=%fused_computation.23 | convolution fusion | flops 49321856 | bytes 6171936 | tf_op jit(solution)/shard_map/dot_general | solution.py:162
  (47 shorter events, 2.4 us)
Async XLA Ops:
  14.8 5.6 %copy-start.1 = (bf16[8,4096]{1,0:T(8,128)(2,1)S(1)}, bf16[8,4096]{1,0:T(8,128)(2,1)}, u32[]{:S(2)}) copy-start(bf16[8,4096]{1,0:T(8,128)(2,1)} %param.9) | copy-start | bytes 196612
  14.8 5.8 %copy-start.6 = (s32[32]{0:T(128)S(1)}, s32[32]{0:T(128)}, u32[]{:S(2)}) copy-start(s32[32]{0:T(128)} %param.15) | copy-start | bytes 388
  14.8 6.9 %copy-start.3 = (bf16[8,512]{1,0:T(8,128)(2,1)S(1)}, bf16[8,512]{1,0:T(8,128)(2,1)}, u32[]{:S(2)}) copy-start(bf16[8,512]{1,0:T(8,128)(2,1)} %param.10) | copy-start | bytes 24580
  14.8 16.9 %copy-start = (bf16[512,512]{1,0:T(8,128)(2,1)S(1)}, bf16[512,512]{1,0:T(8,128)(2,1)}, u32[]{:S(2)}) copy-start(bf16[512,512]{1,0:T(8,128)(2,1)} %param.13) | copy-start | bytes 1572868
  17.1 20.8 %all-to-all-start.2 = ((f32[4,1,512]{2,1,0:T(1,128)}), f32[4,1,512]{2,1,0:T(1,128)S(1)}, u32[]{:S(2)}, u32[]{:S(2)}) async-start(f32[4,1,512]{2,1,0:T(1,128)} %reshape.151), calls=%async_computation.2 | async-start | bytes 16384 | tf_op jit(solution)/shard_map/all_to_all | solution.py:144
  32.7 8.5 %copy-start.4 = (bf16[8,512]{1,0:T(8,128)(2,1)S(1)}, bf16[8,512]{1,0:T(8,128)(2,1)}, u32[]{:S(2)}) copy-start(bf16[8,512]{1,0:T(8,128)(2,1)} %param.11) | copy-start | bytes 24580
  37.9 13.3 %all-to-all-start.1 = ((f32[4,1,512]{2,1,0:T(1,128)}), f32[4,1,512]{2,1,0:T(1,128)S(1)}, u32[]{:S(2)}, u32[]{:S(2)}) async-start(f32[4,1,512]{2,1,0:T(1,128)} %reshape.149), calls=%async_computation.1 | async-start | bytes 16384 | tf_op jit(solution)/shard_map/all_to_all | solution.py:143
  51.2 10.0 %all-to-all-start = ((f32[4,1,32768]{2,1,0:T(1,128)}), f32[4,1,32768]{2,1,0:T(1,128)S(1)}, u32[]{:S(2)}, u32[]{:S(2)}) async-start(f32[4,1,32768]{2,1,0:T(1,128)} %reshape.147), calls=%async_computation | async-start | bytes 1048576 | tf_op jit(solution)/shard_map/all_to_all | solution.py:145
  55.6 18.3 %copy-start.5 = (s32[8]{0:T(128)S(1)}, s32[8]{0:T(128)}, u32[]{:S(2)}) copy-start(s32[8]{0:T(128)} %param.16) | copy-start | bytes 100
  64.9 14.0 %copy-start.2 = (bf16[8,4096]{1,0:T(8,128)(2,1)}, bf16[8,4096]{1,0:T(8,128)(2,1)S(1)}, u32[]{:S(2)}) copy-start(bf16[8,4096]{1,0:T(8,128)(2,1)S(1)} %reshape.142) | copy-start | bytes 196612
where the time goes:
time: 79.5 us; the launch traced here: 78.9 us
  blocking collectives  37 us (47%)
  matrix products  10.1 us (13%)
  starting transfers between devices  9.98 us (13%)
  local copies, waits for them, and re-layouts  9.31 us (12%)
  other arithmetic  5.63 us (7%)
  waiting for transfers between devices  5.21 us (7%)
  between operations  1.63 us (2%)
    all_gather x1, blocking collectives, local(): lax.all_gather(draft_node_queries, 'blk', axis=0, tiled=True)  10.8 us
    all_gather x1, blocking collectives, local(): attention_all = lax.all_gather(attention_own, 'blk', axis=0, tiled=True)  8.98 us
    all_gather x1, blocking collectives, local(): lax.all_gather(draft_node_keys, 'blk', axis=0, tiled=True)  8.65 us
    all_gather x1, blocking collectives, local(): lax.all_gather(draft_node_values, 'blk', axis=0, tiled=True)  8.64 us
    unnamed x24, local copies, waits for them, and re-layouts  6.08 us
    all_to_all x1, waiting for transfers between devices, local(): lax.all_to_all(partial_value[2][None], 'blk', split_axis=1, concat_axis=0...  5.21 us
    dot_general x1, matrix products, local(): lax.dot_general(path_rows, out_weight, (((1,), (1,)), ((), ())), preferre...  5.04 us
    all_to_all x1, starting transfers between devices, local(): lax.all_to_all(partial_value[2][None], 'blk', split_axis=1, concat_axis=0...  3.48 us
  transfers between devices with their start and end apart: 3, of which 1 were waited for; matrix products, arithmetic and copies ran while one was open for 14% of the time, Pallas kernels for 0%

commit v1 on v0

--- a/solution.py
+++ b/solution.py
@@ -152,7 +152,12 @@
         (maxima, totals, weighted), tree_partial(own_queries, keys_all, values_all, own_ancestry)
     )
     attention_own = normalize(partial_value)
-    attention_all = lax.all_gather(attention_own, "blk", axis=0, tiled=True)
+    ring = [attention_own]
+    for hop in range(3):
+        ring.append(lax.ppermute(ring[-1], "blk", [(dev, (dev + 1) % 4) for dev in range(4)]))
+    attention_all = jnp.roll(
+        jnp.concatenate(ring[::-1], axis=0), (lax.axis_index("blk") + 1) * ring[0].shape[0], axis=0
+    )
     picker = (
         accepted_path[:, None] == jnp.arange(draft_node_count, dtype=jnp.int32)[None, :]
     ).astype(jnp.bfloat16)

time: 79.5 us -> 86.9 us (1.093)
  waiting for transfers between devices: 5.21 us -> 18.9 us
  blocking collectives: 37 us -> 28 us
  starting transfers between devices: 9.98 us -> 12.6 us
    ppermute x0 -> x3, waiting for transfers between devices: none -> 13.5 us  [local(): lax.ppermute(ring[-1], 'blk', [(dev, (dev + 1) % 4) for dev in range(4)])]
    all_gather x1 -> x0, blocking collectives: 8.98 us -> none  [local(): attention_all = lax.all_gather(attention_own, 'blk', axis=0, tiled=True)]
    ppermute x0 -> x3, starting transfers between devices: none -> 2.58 us  [local(): lax.ppermute(ring[-1], 'blk', [(dev, (dev + 1) % 4) for dev in range(4)])]
    unnamed x24 -> x31, local copies, waits for them, and re-layouts: 6.08 us -> 6.13 us
  transfers between devices with their start and end apart: 3 -> 6, of which waited for: 1 -> 4; matrix products, arithmetic and copies ran while one was open for 14% -> 13% of each run, Pallas kernels for 0% -> 0%
where the time goes in v1:
time: 86.9 us; the launch traced here: 86.3 us
  blocking collectives  28 us (32%)
  waiting for transfers between devices  18.9 us (22%)
  starting transfers between devices  12.6 us (14%)
  matrix products  10.1 us (12%)
  local copies, waits for them, and re-layouts  9.37 us (11%)
  other arithmetic  5.63 us (6%)
  between operations  1.7 us (2%)
    ppermute x3, waiting for transfers between devices, local(): lax.ppermute(ring[-1], 'blk', [(dev, (dev + 1) % 4) for dev in range(4)])  13.5 us
    all_gather x1, blocking collectives, local(): lax.all_gather(draft_node_queries, 'blk', axis=0, tiled=True)  10.8 us
    all_gather x1, blocking collectives, local(): lax.all_gather(draft_node_keys, 'blk', axis=0, tiled=True)  8.65 us
    all_gather x1, blocking collectives, local(): lax.all_gather(draft_node_values, 'blk', axis=0, tiled=True)  8.64 us
    unnamed x31, local copies, waits for them, and re-layouts  6.13 us
    all_to_all x1, waiting for transfers between devices, local(): lax.all_to_all(partial_value[2][None], 'blk', split_axis=1, concat_axis=0...  5.38 us
    dot_general x1, matrix products, local(): lax.dot_general(path_rows, out_weight, (((1,), (1,)), ((), ())), preferre...  5.05 us
    all_to_all x1, starting transfers between devices, local(): lax.all_to_all(partial_value[2][None], 'blk', split_axis=1, concat_axis=0...  3.48 us
  transfers between devices with their start and end apart: 6, of which 4 were waited for; matrix products, arithmetic and copies ran while one was open for 13% of the time, Pallas kernels for 0%

profile of v1, /device:TPU:0, one launch (start us, length us, event | category | flops | bytes accessed | tf_op | source)
XLA Modules:
  0.0 86.3 jit_solution(14992059178439946525)
XLA Ops:
  1.3 10.8 %all_gather.9 = bf16[32,4096]{1,0:T(8,128)(2,1)S(1)} all-gather(bf16[8,4096]{1,0:T(8,128)(2,1)} %param.9), channel_id=1, replica_groups=mesh['req'=8,'blk'=4] {'blk'}, dimensions={0}, use_global_device_ids=true | all-gather | bytes 327680 | tf_op jit(solution)/shard_map/all_gather | solution.py:127
  12.0 0.5 reshape.137
  12.6 1.3 %copy.73 = bf16[512,512]{0,1:T(8,128)(2,1)S(1)} copy(bf16[512,512]{1,0:T(8,128)(2,1)} %param.12) | data formatting | bytes 1048576 | tf_op args[3]
  13.9 0.9 %bitcast_reduce_fusion = (f32[32,8,8]{0,2,1:T(8,128)S(1)}, f32[8,512,32,8]{1,2,3,0:T(8,128)S(1)}) fusion(pred[512]{0:T(512)(128)(4,1)S(1)} %add_compare_fusion, bf16[512,8,64,1]{0,2,3,1:T(8,128)(2,1)S(1)} %bitcast.84, bf16[32,8,8,64]{3,2,1,0:T(8,128)(2,1)S(1)} %reshape.137), kind=kOutput, calls=%fused_computation.2 | convolution fusion | flops 137361408 | bytes 4989440 | tf_op jit(solution)/shard_map/while/body/eval_jaxpr/mrjz,xrz->mrjx/dot_general | solution.py:49
  14.8 1.4 %fusion.2 = (f32[32,8,8]{0,2,1:T(8,128)S(1)}, bf16[32,8,8,512]{3,0,2,1:T(8,128)(2,1)S(1)}) fusion(f32[8,512,32,8]{1,2,3,0:T(8,128)S(1)} %get-tuple-element.41, f32[32,8,8]{0,2,1:T(8,128)S(1)} %get-tuple-element.39, pred[512]{0:T(512)(128)(4,1)S(1)} %add_compare_fusion), kind=kLoop, calls=%fused_computation.6 | loop fusion | flops 6289408 | bytes 6308352 | tf_op jit(solution)/shard_map/while/body/eval_jaxpr/reduce_sum | solution.py:56
  16.4 0.7 reshape.151
  17.1 3.2 %all-to-all-start.2 = ((f32[4,1,512]{2,1,0:T(1,128)}), f32[4,1,512]{2,1,0:T(1,128)S(1)}, u32[]{:S(2)}, u32[]{:S(2)}) async-start(f32[4,1,512]{2,1,0:T(1,128)} %reshape.151), calls=%async_computation.2 | async-start | bytes 16384 | tf_op jit(solution)/shard_map/all_to_all | solution.py:144
  21.7 8.7 %all_gather.10 = bf16[32,512]{1,0:T(8,128)(2,1)S(1)} all-gather(bf16[8,512]{1,0:T(8,128)(2,1)S(1)} %copy-done.3), channel_id=1, replica_groups=mesh['req'=8,'blk'=4] {'blk'}, dimensions={0}, use_global_device_ids=true | all-gather | bytes 40960 | tf_op jit(solution)/shard_map/all_gather | solution.py:128
  30.5 0.3 fusion.58
  30.9 0.8 copy.75
  31.7 1.0 %copy.76 = bf16[512,512]{0,1:T(8,128)(2,1)} copy(bf16[512,512]{1,0:T(8,128)(2,1)S(1)} %copy-done.1) | data formatting | bytes 1048576 | tf_op args[4]
  32.7 2.4 %fusion.12 = f32[1,32,8,8,64]{4,3,1,2,0:T(8,128)S(1)} fusion(bf16[512,8,64,1]{0,2,3,1:T(8,128)(2,1)} %bitcast.90, bf16[32,8,8,512]{3,0,2,1:T(8,128)(2,1)S(1)} %get-tuple-element.26, f32[32,8,8]{2,0,1:T(8,128)} %copy.75), kind=kOutput, calls=%fused_computation.12 | convolution fusion | flops 134348800 | bytes 3153920 | tf_op jit(solution)/shard_map/while/body/eval_jaxpr/zvle,evt->zvlt/dot_general | solution.py:57
  35.1 0.3 fusion.28
  35.6 0.7 reshape.149
  36.4 1.4 %reshape.147 = f32[4,1,32768]{2,1,0:T(1,128)} reshape(f32[32,1,8,8,64]{4,3,2,1,0:T(8,128)S(1)} %bitcast.83) | data formatting | bytes 1048576
  37.9 3.2 %all-to-all-start.1 = ((f32[4,1,512]{2,1,0:T(1,128)}), f32[4,1,512]{2,1,0:T(1,128)S(1)}, u32[]{:S(2)}, u32[]{:S(2)}) async-start(f32[4,1,512]{2,1,0:T(1,128)} %reshape.149), calls=%async_computation.1 | async-start | bytes 16384 | tf_op jit(solution)/shard_map/all_to_all | solution.py:143
  41.1 8.6 %all_gather.11 = bf16[32,512]{1,0:T(8,128)(2,1)S(1)} all-gather(bf16[8,512]{1,0:T(8,128)(2,1)S(1)} %copy-done.4), channel_id=1, replica_groups=mesh['req'=8,'blk'=4] {'blk'}, dimensions={0}, use_global_device_ids=true | all-gather | bytes 40960 | tf_op jit(solution)/shard_map/all_gather | solution.py:129
  49.9 0.5 broadcast.123
  50.4 0.7 reduce.1
  51.2 3.5 %all-to-all-start = ((f32[4,1,32768]{2,1,0:T(1,128)}), f32[4,1,32768]{2,1,0:T(1,128)S(1)}, u32[]{:S(2)}, u32[]{:S(2)}) async-start(f32[4,1,32768]{2,1,0:T(1,128)} %reshape.147), calls=%async_computation | async-start | bytes 1048576 | tf_op jit(solution)/shard_map/all_to_all | solution.py:145
  54.7 0.7 reduce.2
  56.0 5.4 %all-to-all-done = f32[4,1,32768]{2,1,0:T(1,128)S(1)} async-done(((f32[4,1,32768]{2,1,0:T(1,128)}), f32[4,1,32768]{2,1,0:T(1,128)S(1)}, u32[]{:S(2)}, u32[]{:S(2)}) %all-to-all-start) | async-done | bytes 524320 | tf_op jit(solution)/shard_map/all_to_all | solution.py:145
  61.4 2.1 %reduce = f32[4,32768]{1,0:T(4,128)S(1)} reduce(f32[4,1,32768]{2,1,0:T(1,128)S(1)} %all-to-all-done, f32[]{:T(128)} %broadcast.123), dimensions={1}, to_apply=%all_to_all.12.reduce_sub_computation | reduce | bytes 1048580 | tf_op jit(solution)/shard_map/all_to_all | solution.py:145
  63.6 0.5 reshape.148
  64.1 0.3 multiply_reduce_fusion
  64.5 0.4 fusion.21
  65.1 2.0 %collective-permute-start = (bf16[8,4096]{1,0:T(8,128)(2,1)S(1)}, bf16[8,4096]{1,0:T(8,128)(2,1)S(1)}, u32[]{:S(2)}, u32[]{:S(2)}) collective-permute-start(bf16[8,4096]{1,0:T(8,128)(2,1)S(1)} %reshape.142), channel_id=1, source_target_pairs={{0,1},{1,2},{2,3},{3,0},{4,5},{5,6},{6,7},{7,4},{8,9},{9,10},{10,1... | collective-permute-start | bytes 196616 | tf_op jit(solution)/shard_map/ppermute | solution.py:157
  67.1 3.7 %collective-permute-done = bf16[8,4096]{1,0:T(8,128)(2,1)S(1)} collective-permute-done((bf16[8,4096]{1,0:T(8,128)(2,1)S(1)}, bf16[8,4096]{1,0:T(8,128)(2,1)S(1)}, u32[]{:S(2)}, u32[]{:S(2)}) %collective-permute-start) | collective-permute-done | bytes 65568 | tf_op jit(solution)/shard_map/ppermute | solution.py:157
  70.8 0.6 collective-permute-start.1
  71.4 4.6 %collective-permute-done.1 = bf16[8,4096]{1,0:T(8,128)(2,1)S(1)} collective-permute-done((bf16[8,4096]{1,0:T(8,128)(2,1)S(1)}, bf16[8,4096]{1,0:T(8,128)(2,1)S(1)}, u32[]{:S(2)}, u32[]{:S(2)}) %collective-permute-start.1) | collective-permute-done | bytes 65568 | tf_op jit(solution)/shard_map/ppermute | solution.py:157
  76.0 5.2 %collective-permute-done.2 = bf16[8,4096]{1,0:T(8,128)(2,1)S(1)} collective-permute-done((bf16[8,4096]{1,0:T(8,128)(2,1)S(1)}, bf16[8,4096]{1,0:T(8,128)(2,1)S(1)}, u32[]{:S(2)}, u32[]{:S(2)}) %collective-permute-start.2) | collective-permute-done | bytes 65568 | tf_op jit(solution)/shard_map/ppermute | solution.py:157
  81.3 5.0 %fusion.23 = bf16[8,720]{1,0:T(8,128)(2,1)} fusion(bf16[720,4096]{1,0:T(8,128)(2,1)} %param.17, bf16[64,4096]{1,0:T(8,128)(2,1)S(1)} %constant_dynamic-update-slice_fusion, s32[]{:T(128)S(6)} %select_n.42, s32[8]{0:T(128)S(1)} %copy-done.5), kind=kOutput, calls=%fused_computation.23 | convolution fusion | flops 49321856 | bytes 6172420 | tf_op jit(solution)/shard_map/dot_general | solution.py:167
  (60 shorter events, 3.1 us)
Async XLA Ops:
  14.8 5.6 %copy-start.2 = (bf16[8,4096]{1,0:T(8,128)(2,1)S(1)}, bf16[8,4096]{1,0:T(8,128)(2,1)}, u32[]{:S(2)}) copy-start(bf16[8,4096]{1,0:T(8,128)(2,1)} %param.9) | copy-start | bytes 196612
  14.8 5.8 %copy-start.6 = (s32[32]{0:T(128)S(1)}, s32[32]{0:T(128)}, u32[]{:S(2)}) copy-start(s32[32]{0:T(128)} %param.15) | copy-start | bytes 388
  14.8 6.9 %copy-start.3 = (bf16[8,512]{1,0:T(8,128)(2,1)S(1)}, bf16[8,512]{1,0:T(8,128)(2,1)}, u32[]{:S(2)}) copy-start(bf16[8,512]{1,0:T(8,128)(2,1)} %param.10) | copy-start | bytes 24580
  14.8 16.9 %copy-start.1 = (bf16[512,512]{1,0:T(8,128)(2,1)S(1)}, bf16[512,512]{1,0:T(8,128)(2,1)}, u32[]{:S(2)}) copy-start(bf16[512,512]{1,0:T(8,128)(2,1)} %param.13) | copy-start | bytes 1572868
  17.1 20.8 %all-to-all-start.2 = ((f32[4,1,512]{2,1,0:T(1,128)}), f32[4,1,512]{2,1,0:T(1,128)S(1)}, u32[]{:S(2)}, u32[]{:S(2)}) async-start(f32[4,1,512]{2,1,0:T(1,128)} %reshape.151), calls=%async_computation.2 | async-start | bytes 16384 | tf_op jit(solution)/shard_map/all_to_all | solution.py:144
  32.7 8.5 %copy-start.4 = (bf16[8,512]{1,0:T(8,128)(2,1)S(1)}, bf16[8,512]{1,0:T(8,128)(2,1)}, u32[]{:S(2)}) copy-start(bf16[8,512]{1,0:T(8,128)(2,1)} %param.11) | copy-start | bytes 24580
  37.9 13.3 %all-to-all-start.1 = ((f32[4,1,512]{2,1,0:T(1,128)}), f32[4,1,512]{2,1,0:T(1,128)S(1)}, u32[]{:S(2)}, u32[]{:S(2)}) async-start(f32[4,1,512]{2,1,0:T(1,128)} %reshape.149), calls=%async_computation.1 | async-start | bytes 16384 | tf_op jit(solution)/shard_map/all_to_all | solution.py:143
  51.2 10.2 %all-to-all-start = ((f32[4,1,32768]{2,1,0:T(1,128)}), f32[4,1,32768]{2,1,0:T(1,128)S(1)}, u32[]{:S(2)}, u32[]{:S(2)}) async-start(f32[4,1,32768]{2,1,0:T(1,128)} %reshape.147), calls=%async_computation | async-start | bytes 1048576 | tf_op jit(solution)/shard_map/all_to_all | solution.py:145
  55.7 25.5 %copy-start.5 = (s32[8]{0:T(128)S(1)}, s32[8]{0:T(128)}, u32[]{:S(2)}) copy-start(s32[8]{0:T(128)} %param.16) | copy-start | bytes 100
  65.1 21.3 %copy-start = (bf16[8,4096]{1,0:T(8,128)(2,1)}, bf16[8,4096]{1,0:T(8,128)(2,1)S(1)}, u32[]{:S(2)}) copy-start(bf16[8,4096]{1,0:T(8,128)(2,1)S(1)} %reshape.142) | copy-start | bytes 196612
  65.1 5.7 %collective-permute-start = (bf16[8,4096]{1,0:T(8,128)(2,1)S(1)}, bf16[8,4096]{1,0:T(8,128)(2,1)S(1)}, u32[]{:S(2)}, u32[]{:S(2)}) collective-permute-start(bf16[8,4096]{1,0:T(8,128)(2,1)S(1)} %reshape.142), channel_id=1, source_target_pairs={{0,1},{1,2},{2,3},{3,0},{4,5},{5,6},{6,7},{7,4},{8,9},{9,10},{10,1... | collective-permute-start | bytes 196616 | tf_op jit(solution)/shard_map/ppermute | solution.py:157
  70.8 5.2 %collective-permute-start.1 = (bf16[8,4096]{1,0:T(8,128)(2,1)S(1)}, bf16[8,4096]{1,0:T(8,128)(2,1)S(1)}, u32[]{:S(2)}, u32[]{:S(2)}) collective-permute-start(bf16[8,4096]{1,0:T(8,128)(2,1)S(1)} %collective-permute-done), channel_id=1, source_target_pairs={{0,1},{1,2},{2,3},{3,0},{4,5},{5,6},{6,7},{7,4},{8,9},{9,10},{10,1... | collective-permute-start | bytes 196616 | tf_op jit(solution)/shard_map/ppermute | solution.py:157
  76.0 5.2 %collective-permute-start.2 = (bf16[8,4096]{1,0:T(8,128)(2,1)S(1)}, bf16[8,4096]{1,0:T(8,128)(2,1)S(1)}, u32[]{:S(2)}, u32[]{:S(2)}) collective-permute-start(bf16[8,4096]{1,0:T(8,128)(2,1)S(1)} %collective-permute-done.1), channel_id=1, source_target_pairs={{0,1},{1,2},{2,3},{3,0},{4,5},{5,6},{6,7},{7,4},{8,9},{9,10},{10,1... | collective-permute-start | bytes 196616 | tf_op jit(solution)/shard_map/ppermute | solution.py:157
